TPU v7x, 32 devices: a whole 2x2x4 slice. The times are simulated.
32 devices in a mesh: blk: 8 (over y, x, core), grp: 4 (over z).
Axes of the slice: x: 2, y: 2, z: 4, core: 2. Of those that a mesh axis runs over, the one named last changes fastest.
Arguments:
- source: float32 [2048, 128], P(('blk', 'grp')), may hold values from -3 to 3
- target: float32 [2048, 128], P(('blk', 'grp')), may hold values from -3 to 3
- source_mass: float32 [2048], P(('blk', 'grp')), may hold values from 0.25 to 4
- target_mass: float32 [2048], P(('blk', 'grp')), may hold values from 0.25 to 4
Outputs:
- source_dual: float32 [2048], P(('blk', 'grp'))
- target_dual: float32 [2048], P(('blk', 'grp'))
All inputs are finite; a program needn't handle non-finite values.
Results may differ from a plain program's by a relative error of at most 0.0003.
Values sent between devices are 32-bit elements; how exact they have to be, the bound alone decides.
A program may use at most 64 MiB of HBM per device.

v0:
```python
import functools
import math

import jax
import jax.numpy as jnp
from jax import lax
from jax.experimental import pallas as pl
from jax.experimental.pallas import tpu as pltpu
from jax.sharding import PartitionSpec as P

ITERS = 8
eps = 0.5
LOG2E = math.log2(math.e)
ALPHA = LOG2E / eps
LANES = 128
SUB = 8
OCT = 8
PIECES = 2
UNIT = 4
GROUPS = 32
MESH = pl.DeviceIdType.MESH
BUDGET = 36 * 2**20


def exp2(x):
    return jnp.exp2(x)


def log2(x):
    return jnp.log2(x)


def lse_blocks(pairs):
    top = functools.reduce(jnp.maximum, [m for m, _ in pairs])
    if len(pairs) == 1:
        return pairs[0]
    return top, sum(s * exp2(m - top) for m, s in pairs)


def kernel(blk_n, grp_n, part, count, pieces, src_ref, tgt_ref, smass_ref, tmass_ref, out_ref,
           src_all, tgt_all, spack, tpack, cost, tcat, u, v, loga, logb, part_lse, piece_top, piece_sum,
           s_send, f_send, s_recv, t_send, t_recv, x_send, x_recv):
    n_dev = blk_n * grp_n
    rep = LANES // count
    chunks = n_dev // rep
    quads = blk_n // part
    t_dev = quads * grp_n
    nj = t_dev * count
    b, g = lax.axis_index("blk"), lax.axis_index("grp")
    me = b * grp_n + g
    q, p = b // part, b % part
    mine_t = q * grp_n + g

    peers = n_dev // OCT
    z, low = (b // OCT) * grp_n + g, b % OCT

    def flip(i, bit):
        return i + bit * (1 - 2 * ((i // bit) % 2))

    def place(step, bits):
        peer = lax.rem(z + step, peers)
        home = low
        for bit in (1, 2, 4):
            if bits & bit:
                home = flip(home, bit)
        return ((peer // grp_n) * OCT + home) * grp_n + peer % grp_n

    barrier = pltpu.get_barrier_semaphore()

    def greet(step, _):
        other = place(step, 0)
        pl.semaphore_signal(barrier, inc=1, device_id=(other // grp_n, other % grp_n), device_id_type=MESH)
        return 0

    lax.fori_loop(1, peers, greet, 0)

    def greet_part(step, _):
        other = q * part + lax.rem(p + step, part)
        pl.semaphore_signal(barrier, inc=1, device_id=(other, g), device_id_type=MESH)
        return 0

    lax.fori_loop(1, part, greet_part, 0)

    lane = lax.broadcasted_iota(jnp.int32, (1, LANES), 1)
    here = lane // count == me % rep

    def pack(ref, mass_ref, out, scale):
        out[0:count, :] = ref[...] * scale
        row = log2(mass_ref[...])
        row = jnp.where(here, jnp.concatenate([row] * rep, axis=1), 0.0)
        out[count : count + SUB, :] = jnp.broadcast_to(row, (SUB, LANES))

    pack(src_ref, smass_ref, spack, 2.0 * ALPHA)
    pack(tgt_ref, tmass_ref, tpack, 1.0)
    src_all[pl.ds(me, 1)] = spack[...][None]
    tgt_all[pl.ds(mine_t, 1)] = tpack[...][None]
    pl.semaphore_wait(barrier, peers + part - 2)

    def tgt_copy(slot, r, sem_slot):
        return pltpu.make_async_remote_copy(
            src_ref=tpack, dst_ref=tgt_all.at[slot],
            send_sem=t_send.at[r], recv_sem=t_recv.at[sem_slot],
            device_id=((r // grp_n) * part + p, r % grp_n), device_id_type=MESH)

    def src_copy(slot, d, step):
        return pltpu.make_async_remote_copy(
            src_ref=spack, dst_ref=src_all.at[slot],
            send_sem=s_send.at[step], recv_sem=s_recv.at[slot],
            device_id=(d // grp_n, d % grp_n), device_id_type=MESH)

    def push(slot, way):
        return pltpu.make_async_remote_copy(
            src_ref=src_all.at[slot], dst_ref=src_all.at[slot],
            send_sem=f_send.at[way, slot], recv_sem=s_recv.at[slot],
            device_id=(flip(b, 2 ** way), g), device_id_type=MESH)

    def arrive(slot):
        src_copy(slot, me, 0).wait_recv()

    def send_t(step, _):
        tgt_copy(mine_t, lax.rem(mine_t + step, t_dev), mine_t).start()
        return 0

    def send_s(step, _):
        src_copy(me, place(step, 0), step).start()
        return 0

    def wait_t(step, _):
        r = lax.rem(mine_t + step, t_dev)
        tgt_copy(mine_t, r, mine_t).wait_send()
        tgt_copy(r, r, r).wait_recv()
        return 0

    def make_cost(k):
        blocks = [src_all[k * rep + i, 0:count, :] for i in range(rep)]
        masses = sum(src_all[k * rep + i, count : count + 1, :] for i in range(rep))
        loga[pl.ds(k, 1), :] = masses
        cost[k] = lax.dot_general(
            tcat[...], jnp.concatenate(blocks, axis=0), (((1,), (1,)), ((), ())),
            precision=lax.Precision.HIGHEST, preferred_element_type=jnp.float32)

    def costs(bits):
        home = low
        for bit in (1, 2, 4):
            if bits & bit:
                home = flip(home, bit)
        per = grp_n // rep

        def one(i, _):
            make_cost(((i // per) * OCT + home) * per + i % per)
            return 0

        lax.fori_loop(0, peers // rep, one, 0)

    for way in range(3):
        push(me, way).start()
    lax.fori_loop(1, peers, send_s, 0)
    lax.fori_loop(1, t_dev, send_t, 0)

    def relay(bits, ways):
        def go(step, _):
            slot = place(step, bits)
            arrive(slot)
            for way in ways:
                push(slot, way).start()
            return 0
        return go

    half = peers // 2
    lax.fori_loop(1, peers, relay(0, (1, 2, 0)), 0)
    lax.fori_loop(1, t_dev, wait_t, 0)

    eye = (lax.broadcasted_iota(jnp.int32, (count, LANES), 1) % count
           == lax.broadcasted_iota(jnp.int32, (count, LANES), 0))
    for r in range(t_dev):
        rows = slice(r * count, (r + 1) * count)
        block = tgt_all[r, 0:count, :]
        tcat[rows, :] = block
        mass = jnp.sum(jnp.where(eye, tgt_all[r, count : count + 1, :], 0.0), axis=1, keepdims=True)
        square = jnp.sum(block * block, axis=1, keepdims=True)
        logb[rows, :] = jnp.broadcast_to(mass, (count, LANES))
        u[rows, :] = jnp.broadcast_to(mass - ALPHA * square, (count, LANES))

    lax.fori_loop(0, half, relay(2, (2, 0)), 0)
    lax.fori_loop(0, half, relay(4, (0,)), 0)
    lax.fori_loop(half, peers, relay(4, (1, 0)), 0)
    lax.fori_loop(half, peers, relay(2, (0,)), 0)
    costs(0)
    costs(2)
    costs(4)
    lax.fori_loop(0, peers, relay(6, (0,)), 0)
    costs(6)
    for bits in (1, 3, 5, 7):
        lax.fori_loop(0, peers, relay(bits, ()), 0)
        costs(bits)

    def sent_s(step, _):
        src_copy(me, place(step, 0), step).wait_send()
        return 0

    def sent(bits, ways):
        def go(step, _):
            for way in ways:
                push(place(step, bits), way).wait_send()
            return 0
        return go

    lax.fori_loop(1, peers, sent_s, 0)
    lax.fori_loop(0, peers, sent(0, (0, 1, 2)), 0)
    lax.fori_loop(0, half, sent(2, (2, 0)), 0)
    lax.fori_loop(0, half, sent(4, (0,)), 0)
    lax.fori_loop(half, peers, sent(4, (1, 0)), 0)
    lax.fori_loop(half, peers, sent(2, (0,)), 0)
    lax.fori_loop(0, peers, sent(6, (0,)), 0)

    rows_at_once = min(nj, 128)
    size = chunks // pieces
    unit = math.gcd(size, UNIT)

    def source_unit(slot, c, k0):
        tops, totals = [], []
        for h in range(unit):
            pairs = []
            for r in range(0, nj, rows_at_once):
                x = cost[c * size + k0 + h, r : r + rows_at_once, :] + u[r : r + rows_at_once, :]
                x = x.reshape(rows_at_once // SUB, SUB, LANES)
                m = jnp.max(x, axis=0)
                pairs.append((m, jnp.sum(exp2(x - m[None]), axis=0)))
            m, s = lse_blocks(pairs)
            top = jnp.max(m, axis=0, keepdims=True)
            tops.append(top)
            totals.append(jnp.sum(s * exp2(m - top), axis=0, keepdims=True))
        part_lse[slot, c, p, pl.ds(k0, unit), :] = (
            jnp.concatenate(tops, axis=0) + log2(jnp.concatenate(totals, axis=0)))

    groups = math.gcd(nj // SUB, GROUPS)

    def target_rows(c, i):
        for h in range(groups):
            rows = pl.ds(pl.multiple_of((i * groups + h) * SUB, SUB), SUB)
            pairs = []
            for k0 in range(c * size, (c + 1) * size, 16):
                x = [cost[k, rows, :] + v[k : k + 1, :] for k in range(k0, min(k0 + 16, (c + 1) * size))]
                m = functools.reduce(jnp.maximum, x)
                pairs.append((m, sum(exp2(y - m) for y in x)))
            m, s = lse_blocks(pairs)
            if c < pieces - 1:
                piece_top[c, rows, :] = m
                piece_sum[c, rows, :] = s
                continue
            m, s = lse_blocks([(m, s)] + [(piece_top[i2, rows, :], piece_sum[i2, rows, :]) for i2 in range(c)])
            top = jnp.max(m, axis=1, keepdims=True)
            total = jnp.sum(s * exp2(m - top), axis=1, keepdims=True)
            u[rows, :] = logb[rows, :] - (top + log2(total))

    def swap(slot, c, writer, other, sem_at):
        return pltpu.make_async_remote_copy(
            src_ref=part_lse.at[slot, c, p], dst_ref=part_lse.at[slot, c, writer],
            send_sem=x_send.at[slot, c, other], recv_sem=x_recv.at[slot, c, sem_at],
            device_id=(q * part + other, g), device_id_type=MESH)

    def iteration(t, _):
        slot = lax.rem(t, 2)

        for c in range(pieces):
            def one(i, _):
                source_unit(slot, c, i * unit)
                return 0

            if size == unit:
                source_unit(slot, c, 0)
            else:
                lax.fori_loop(0, size // unit, one, 0)
            for step in range(1, part):
                swap(slot, c, p, lax.rem(p + step, part), p).start()
        for c in range(pieces):
            for step in range(1, part):
                other = lax.rem(p + step, part)
                swap(slot, c, other, other, other).wait_recv()
            parts = [part_lse[slot, c, i] for i in range(part)]
            top = functools.reduce(jnp.maximum, parts)
            rows = slice(c * size, (c + 1) * size)
            v[rows, :] = loga[rows, :] - (top + log2(sum(exp2(y - top) for y in parts)))

            def two(i, _):
                target_rows(c, i)
                return 0

            lax.fori_loop(0, nj // (SUB * groups), two, 0)
        for c in range(pieces):
            for step in range(1, part):
                swap(slot, c, p, lax.rem(p + step, part), p).wait_send()
        return 0

    lax.fori_loop(0, ITERS, iteration, 0)

    def to_lanes(column):
        return jnp.sum(jnp.where(eye, column, 0.0), axis=0, keepdims=True)

    src = src_ref[...]
    row = pl.ds(me // rep, 1)
    lse_s = loga[row, :] - v[row, :]
    first = to_lanes(jnp.sum(src * src, axis=1, keepdims=True)) - (1.0 / ALPHA) * lse_s
    tgt = tgt_ref[...]
    own = pl.ds(pl.multiple_of(mine_t * count, count), count)
    lse_t = logb[own, :] - u[own, :]
    second = to_lanes(jnp.sum(tgt * tgt, axis=1, keepdims=True) - (1.0 / ALPHA) * lse_t)
    picked = first[:, 0:count]
    for i in range(1, rep):
        picked = jnp.where(me % rep == i, first[:, i * count : (i + 1) * count], picked)
    out_ref[0:1, 0:count] = picked
    out_ref[1:2, 0:count] = second[:, 0:count]


def solution(mesh):
    blk_n, grp_n = mesh.shape["blk"], mesh.shape["grp"]
    n_dev = blk_n * grp_n

    def per_device(source, target, source_mass, target_mass):
        count, width = source.shape
        points = n_dev * count
        part = OCT
        while part < blk_n and (points // part) * points * 4 > BUDGET:
            part *= 2
        nj = points // part
        t_dev = n_dev // part
        chunks = points // LANES
        pieces = math.gcd(chunks, PIECES)
        wide = count + SUB
        f32 = jnp.float32
        vmem = pl.BlockSpec(memory_space=pltpu.VMEM)
        dma = pltpu.SemaphoreType.DMA
        out = pl.pallas_call(
            functools.partial(kernel, blk_n, grp_n, part, count, pieces),
            out_shape=jax.ShapeDtypeStruct((2, count), f32),
            in_specs=[vmem] * 4,
            out_specs=vmem,
            scratch_shapes=[
                pltpu.VMEM((n_dev, wide, width), f32),
                pltpu.VMEM((t_dev, wide, width), f32),
                pltpu.VMEM((wide, width), f32),
                pltpu.VMEM((wide, width), f32),
                pltpu.VMEM((chunks, nj, LANES), f32),
                pltpu.VMEM((nj, width), f32),
                pltpu.VMEM((nj, LANES), f32),
                pltpu.VMEM((chunks, LANES), f32),
                pltpu.VMEM((chunks, LANES), f32),
                pltpu.VMEM((nj, LANES), f32),
                pltpu.VMEM((2, pieces, part, chunks // pieces, LANES), f32),
                pltpu.VMEM((pieces, nj, LANES), f32),
                pltpu.VMEM((pieces, nj, LANES), f32),
                dma((n_dev // OCT,)), dma((3, n_dev)), dma((n_dev,)),
                dma((t_dev,)), dma((t_dev,)),
                dma((2, pieces, part)), dma((2, pieces, part)),
            ],
            compiler_params=pltpu.CompilerParams(
                collective_id=0, has_side_effects=True, vmem_limit_bytes=62 * 2**20),
        )(source, target, source_mass.reshape(1, count), target_mass.reshape(1, count))
        return out[0], out[1]

    both = P(("blk", "grp"))
    return jax.shard_map(
        per_device,
        mesh=mesh,
        in_specs=(P(("blk", "grp"), None), P(("blk", "grp"), None), both, both),
        out_specs=(both, both),
        check_vma=False,
    )
```

profile of v0, /device:TPU:1, one launch (start us, length us, event | category | flops | bytes accessed | tf_op | source)
XLA Modules:
  0.0 59.2 jit_solution(18015907910864778505)
XLA Ops:
  0.6 57.3 %shard_map.59 = f32[2,64]{1,0:T(2,128)} custom-call(f32[64,128]{1,0:T(8,128)} %src_ref.1, f32[64,128]{1,0:T(8,128)} %tgt_ref.1, f32[1,64]{1,0:T(1,128)} %bitcast.6, f32[1,64]{1,0:T(1,128)} %bitcast.7), custom_call_target="tpu_custom_call" | custom-call | tf_op jit(solution)/shard_map/pallas_call | solution.py:333
  58.0 1.3 %slice_bitcast_fusion = (f32[64]{0:T(128)}, f32[64]{0:T(128)}) fusion(f32[2,64]{1,0:T(2,128)} %shard_map.59), kind=kLoop, calls=%fused_computation | loop fusion | bytes 1024 | tf_op jit(solution)/shard_map/squeeze | solution.py:359
where the time goes:
time: 59.8 us; the launch traced here: 59.2 us
  Pallas kernels  57.3 us (96%)
  local copies, waits for them, and re-layouts  1.25 us (2%)
  between operations  0.64 us (1%)
    pallas_call x1, Pallas kernels, per_device(): pl.pallas_call(functools.partial(kernel, blk_n, grp_n, part, count, piece...  57.3 us
    squeeze x1, local copies, waits for them, and re-layouts, per_device(): return (out[0], out[1])  1.25 us

commit v1 on v0

--- a/solution.py
+++ b/solution.py
@@ -37,7 +37,7 @@
     return top, sum(s * exp2(m - top) for m, s in pairs)
 
 
-def kernel(blk_n, grp_n, part, count, pieces, src_ref, tgt_ref, smass_ref, tmass_ref, out_ref,
+def wide_kernel(blk_n, grp_n, part, count, pieces, src_ref, tgt_ref, smass_ref, tmass_ref, out_ref,
            src_all, tgt_all, spack, tpack, cost, tcat, u, v, loga, logb, part_lse, piece_top, piece_sum,
            s_send, f_send, s_recv, t_send, t_recv, x_send, x_recv):
     n_dev = blk_n * grp_n
@@ -312,11 +312,549 @@
     out_ref[1:2, 0:count] = second[:, 0:count]
 
 
+FLOOR = 2.0**-40
+GROUP = 8
+MROWS = 256
+
+
+def split(x):
+    hi = x.astype(jnp.bfloat16)
+    return hi, (x - hi.astype(jnp.float32)).astype(jnp.bfloat16)
+
+
+def xor(x, y):
+    return sum(((x // bit + y // bit) % 2) * bit for bit in (1, 2, 4))
+
+
+def mix(z, step, peers):
+    other = 0
+    bit = 1
+    while bit < peers:
+        other = other + ((z // bit + step // bit) % 2) * bit
+        bit *= 2
+    return other
+
+
+def chip_kernel(grp_n, count, src_ref, tgt_ref, smass_ref, tmass_ref, out_ref, src_hbm, tgt_hbm,
+                src_all, tgt_all, spack, tpack, tcat, expo, bvec, cvec, own, msg, msg_in,
+                part, part_in, rho, mass_a, scale, tops,
+                s_send, f_send, s_recv, t_send, g_send, t_recv, m_send, m_recv, x_send, x_recv, h_sem):
+    wide = count + 1
+    lines = OCT // 2
+    slots_t = lines * grp_n
+    nt = slots_t * count
+    groups = nt // SUB
+    width = grp_n * count
+    halves = width // LANES
+    rep = LANES // count
+    chunks = OCT * halves
+    b, g = lax.axis_index("blk"), lax.axis_index("grp")
+    me = b * grp_n + g
+    core = b % 2
+    mate = b + 1 - 2 * core
+
+    def side(bits):
+        return xor(b, bits)
+
+    def slot_of(home, z):
+        return home * grp_n + z
+
+    barrier = pltpu.get_barrier_semaphore()
+
+    def greet(step, _):
+        pl.semaphore_signal(barrier, inc=1, device_id=(b, mix(g, step, grp_n)), device_id_type=MESH)
+        return 0
+
+    lax.fori_loop(1, grp_n, greet, 0)
+    for bits in (1, 2, 4):
+        pl.semaphore_signal(barrier, inc=1, device_id=(side(bits), g), device_id_type=MESH)
+
+    lane = lax.broadcasted_iota(jnp.int32, (1, LANES), 1)
+
+    def pack(ref, mass_ref, out, place):
+        out[0:count, :] = ref[...]
+        row = jnp.concatenate([mass_ref[...]] * rep, axis=1)
+        out[count:wide, :] = jnp.where(lane // count == place, row, 0.0)
+
+    pack(src_ref, smass_ref, spack, me % rep)
+    pack(tgt_ref, tmass_ref, tpack, 0)
+    src_all[pl.ds(me, 1)] = spack[...][None]
+    tgt_all[pl.ds(me, 1)] = tpack[...][None]
+    pl.semaphore_wait(barrier, grp_n + 2)
+
+    def line(pk, buf, send, recv, step):
+        return pltpu.make_async_remote_copy(
+            src_ref=pk, dst_ref=buf.at[me], send_sem=send.at[step], recv_sem=recv.at[me],
+            device_id=(b, mix(g, step, grp_n)), device_id_type=MESH)
+
+    def push(buf, send, recv, slot, way):
+        return pltpu.make_async_remote_copy(
+            src_ref=buf.at[slot], dst_ref=buf.at[slot], send_sem=send.at[way, slot], recv_sem=recv.at[slot],
+            device_id=(side(2 ** way), g), device_id_type=MESH)
+
+    def first(pk, buf, send, recv, way):
+        return pltpu.make_async_remote_copy(
+            src_ref=pk, dst_ref=buf.at[me], send_sem=send.at[way, me], recv_sem=recv.at[me],
+            device_id=(side(2 ** way), g), device_id_type=MESH)
+
+    def s_push(slot, way):
+        return push(src_all, f_send, s_recv, slot, way)
+
+    def t_push(slot, way):
+        return push(tgt_all, g_send, t_recv, slot, way)
+
+    def s_arrive(slot):
+        s_push(slot, 0).wait_recv()
+
+    def t_arrive(slot):
+        t_push(slot, 0).wait_recv()
+
+    for way in (1, 2):
+        first(tpack, tgt_all, g_send, t_recv, way).start()
+
+    def send_line(pk, buf, send, recv):
+        def go(step, _):
+            line(pk, buf, send, recv, step).start()
+            return 0
+        lax.fori_loop(1, grp_n, go, 0)
+
+    send_line(tpack, tgt_all, t_send, t_recv)
+    for way in (1, 2, 0):
+        first(spack, src_all, f_send, s_recv, way).start()
+    send_line(spack, src_all, s_send, s_recv)
+
+    def relay(pushes, arrive, bits, ways, lo, hi):
+        def go(step, _):
+            slot = slot_of(side(bits), mix(g, step, grp_n))
+            arrive(slot)
+            for way in ways:
+                pushes(slot, way).start()
+            return 0
+        lax.fori_loop(lo, hi, go, 0)
+
+    eye = (lax.broadcasted_iota(jnp.int32, (count, LANES), 1)
+           == lax.broadcasted_iota(jnp.int32, (count, LANES), 0))
+
+    def prepare(bits):
+        home = side(bits)
+        for z in range(grp_n):
+            slot = slot_of(home, z)
+            rows = pl.ds(pl.multiple_of(((home // 2) * grp_n + z) * count, count), count)
+            block = tgt_all[slot, 0:count, :]
+            hi, lo = split(block)
+            tcat[rows, 0:LANES] = hi
+            tcat[rows, LANES : 2 * LANES] = lo
+            mass = jnp.sum(jnp.where(eye, tgt_all[slot, count:wide, :], 0.0), axis=1, keepdims=True)
+            square = jnp.sum(block * block, axis=1, keepdims=True)
+            mass = jnp.broadcast_to(mass, (count, LANES))
+            bvec[rows, :] = mass
+            cvec[rows, :] = log2(mass) - ALPHA * square
+
+    half = grp_n // 2
+    relay(t_push, t_arrive, 0, (1, 2), 1, grp_n)
+    relay(s_push, s_arrive, 0, (1, 2, 0), 1, grp_n)
+    prepare(0)
+    relay(t_push, t_arrive, 2, (2,), 0, half)
+    relay(t_push, t_arrive, 4, (), 0, half)
+    relay(t_push, t_arrive, 4, (1,), half, grp_n)
+    relay(t_push, t_arrive, 2, (), half, grp_n)
+    relay(s_push, s_arrive, 2, (2, 0), 0, half)
+    relay(s_push, s_arrive, 4, (0,), 0, half)
+    relay(s_push, s_arrive, 4, (1, 0), half, grp_n)
+    relay(s_push, s_arrive, 2, (0,), half, grp_n)
+    prepare(2)
+    prepare(4)
+    relay(t_push, t_arrive, 6, (), 0, grp_n)
+    prepare(6)
+
+    def tell(kb):
+        return pltpu.make_async_remote_copy(
+            src_ref=msg.at[kb], dst_ref=msg_in.at[kb], send_sem=m_send.at[kb], recv_sem=m_recv.at[kb],
+            device_id=(mate, g), device_id_type=MESH)
+
+    def build(kb):
+        s = jnp.concatenate([src_all[kb * grp_n + z, 0:count, :] for z in range(grp_n)], axis=0) * (2.0 * ALPHA)
+        hi, lo = split(s)
+        twice = jnp.concatenate([hi, hi], axis=1)
+        dims = (((1,), (1,)), ((), ()))
+        top = None
+        for r in range(0, nt, MROWS):
+            x = (lax.dot_general(tcat[r : r + MROWS, :], twice, dims, preferred_element_type=jnp.float32)
+                 + lax.dot_general(tcat[r : r + MROWS, 0:LANES], lo, dims, preferred_element_type=jnp.float32))
+            c = cvec[r : r + MROWS, :].reshape(MROWS // SUB, SUB, LANES)
+            tall = []
+            for h in range(halves):
+                y = x[:, h * LANES : (h + 1) * LANES].reshape(MROWS // SUB, SUB, LANES) + c
+                expo[r // SUB : (r + MROWS) // SUB, kb * halves + h] = y
+                tall.append(jnp.max(y, axis=0))
+            top = tall if top is None else [jnp.maximum(p, q) for p, q in zip(top, tall)]
+        for h in range(halves):
+            m = jnp.max(top[h], axis=0, keepdims=True)
+            total = jnp.zeros((SUB, LANES), jnp.float32)
+            for r in range(0, nt, MROWS):
+                at = slice(r // SUB, (r + MROWS) // SUB)
+                y = exp2(expo[at, kb * halves + h] - m[None])
+                expo[at, kb * halves + h] = y
+                total = total + jnp.sum(y, axis=0)
+            msg[kb, h : h + 1, :] = m
+            msg[kb, halves + h : halves + h + 1, :] = jnp.sum(total, axis=0, keepdims=True)
+            mass = sum(src_all[kb * grp_n + h * rep + i, count:wide, :] for i in range(rep))
+            mass_a[pl.ds(kb * halves + h, 1), :] = mass
+        tell(kb).start()
+
+    def even(i, _):
+        build(side(2 * i))
+        return 0
+
+    def odd(i, _):
+        home = side(2 * i + 1)
+
+        def go(z, _):
+            s_arrive(slot_of(home, z))
+            return 0
+
+        lax.fori_loop(0, grp_n, go, 0)
+        build(home)
+        return 0
+
+    lax.fori_loop(0, 3, even, 0)
+    relay(s_push, s_arrive, 6, (0,), 0, grp_n)
+    lax.fori_loop(3, 4, even, 0)
+    lax.fori_loop(0, 4, odd, 0)
+
+    def hand(i, _):
+        t_push(slot_of(2 * (i // grp_n) + core, i % grp_n), 0).start()
+        return 0
+
+    lax.fori_loop(0, slots_t, hand, 0)
+    copy_s = pltpu.make_async_copy(src_all, src_hbm, h_sem.at[0])
+    copy_s.start()
+
+    def told(kb, _):
+        tell(kb).wait()
+        rows = pl.ds(kb * halves, halves)
+        m, s = msg[kb, 0:halves, :], msg[kb, halves : 2 * halves, :]
+        m2, s2 = msg_in[kb, 0:halves, :], msg_in[kb, halves : 2 * halves, :]
+        top = jnp.maximum(m, m2)
+        q = exp2(m - top)
+        total = q * s + exp2(m2 - top) * s2
+        tops[rows, :] = top
+        scale[rows, :] = q
+        rho[rows, :] = q * (mass_a[rows, :] / total)
+        return 0
+
+    lax.fori_loop(0, OCT, told, 0)
+
+    def row_sum(r, weights):
+        terms = [expo[r, k] * weights[k] for k in range(chunks)]
+        while len(terms) > 1:
+            terms = [p + q for p, q in zip(terms[::2], terms[1::2])] + terms[len(terms) // 2 * 2 :]
+        return jnp.broadcast_to(jnp.sum(terms[0], axis=1, keepdims=True), (SUB, LANES))
+
+    def weights():
+        return [jnp.broadcast_to(rho[k : k + 1, :], (SUB, LANES)) for k in range(chunks)]
+
+    blocks = groups // GROUP
+
+    def swap(slot):
+        return pltpu.make_async_remote_copy(
+            src_ref=part.at[slot], dst_ref=part_in.at[slot], send_sem=x_send.at[slot], recv_sem=x_recv.at[slot],
+            device_id=(mate, g), device_id_type=MESH)
+
+    def iteration(t, low):
+        low_s, low_r = low
+        slot = lax.rem(t, 2)
+        ws = weights()
+
+        def sums(i):
+            return [row_sum(i * GROUP + h, ws) for h in range(GROUP)]
+
+        def spread(i, tot, acc, low):
+            acc = list(acc)
+            for h in range(GROUP):
+                r = i * GROUP + h
+                low = jnp.minimum(low, tot[h])
+                w = bvec[pl.ds(pl.multiple_of(r * SUB, SUB), SUB), :] / tot[h]
+                for k in range(chunks):
+                    acc[k] = acc[k] + expo[r, k] * w
+            return tuple(acc), low
+
+        def body(i, carry):
+            tot, acc, low = carry
+            fresh = sums(i)
+            acc, low = spread(i - 1, tot, acc, low)
+            return tuple(fresh), acc, low
+
+        zero = jnp.zeros((SUB, LANES), jnp.float32)
+        tot, acc, low_r = lax.fori_loop(1, blocks, body, (tuple(sums(0)), (zero,) * chunks, low_r))
+        acc, low_r = spread(blocks - 1, tot, acc, low_r)
+        mine = jnp.concatenate([jnp.sum(x, axis=0, keepdims=True) for x in acc], axis=0) * scale[...]
+        part[slot, 0:chunks, :] = mine
+        part[slot, chunks : chunks + SUB, :] = low_r
+        swap(slot).start()
+        swap(slot).wait_recv()
+        total = mine + part_in[slot, 0:chunks, :]
+        low_r = jnp.minimum(low_r, part_in[slot, chunks : chunks + SUB, :])
+        low_s = jnp.minimum(low_s, total)
+        rho[...] = scale[...] * (mass_a[...] / total)
+        tops_now = tops[...] + log2(total)
+        own[...] = tops_now
+        swap(slot).wait_send()
+        return low_s, low_r
+
+    low_s, low_r = lax.fori_loop(
+        1, ITERS, iteration,
+        (jnp.full((chunks, LANES), 1.0, jnp.float32), jnp.full((SUB, LANES), 1.0, jnp.float32)))
+
+    def wait_hand(i, _):
+        s = slot_of(2 * (i // grp_n) + core, i % grp_n)
+        o = slot_of(2 * (i // grp_n) + 1 - core, i % grp_n)
+        t_push(s, 0).wait_send()
+        t_arrive(o)
+        return 0
+
+    ws = weights()
+    base = ((b // 2) * grp_n + g) * (count // SUB)
+    per = count // SUB
+    tot = [row_sum(base + h, ws) for h in range(per)]
+    for h in range(per):
+        low_r = jnp.minimum(low_r, tot[h])
+    mine = pl.ds(pl.multiple_of(base * SUB, count), count)
+    g_col = (1.0 / ALPHA) * (log2(bvec[mine, :]) - log2(jnp.concatenate(tot, axis=0)))
+
+    def to_lanes(column):
+        return jnp.sum(jnp.where(eye, column, 0.0), axis=0, keepdims=True)
+
+    src = src_ref[...]
+    square = jnp.sum(src * src, axis=1, keepdims=True)
+    eye2 = (lax.broadcasted_iota(jnp.int32, (count, LANES), 1) % count
+            == lax.broadcasted_iota(jnp.int32, (count, LANES), 0))
+    norm = jnp.sum(jnp.where(eye2, square, 0.0), axis=0, keepdims=True)
+    full = norm - (1.0 / ALPHA) * own[pl.ds(me // rep, 1), :]
+    picked = full[:, 0:count]
+    for i in range(1, rep):
+        picked = jnp.where(me % rep == i, full[:, i * count : (i + 1) * count], picked)
+    out_ref[0:1, 0:count] = picked
+    out_ref[1:2, 0:count] = to_lanes(g_col)[:, 0:count]
+    least = jnp.minimum(jnp.min(low_s, axis=0, keepdims=True), jnp.min(low_r, axis=0, keepdims=True))
+    out_ref[2:3, :] = least
+
+    lax.fori_loop(0, slots_t, wait_hand, 0)
+    copy_t = pltpu.make_async_copy(tgt_all, tgt_hbm, h_sem.at[1])
+    copy_t.start()
+
+    def sent_line(step, _):
+        line(tpack, tgt_all, t_send, t_recv, step).wait_send()
+        line(spack, src_all, s_send, s_recv, step).wait_send()
+        return 0
+
+    lax.fori_loop(1, grp_n, sent_line, 0)
+    for way in (1, 2):
+        first(tpack, tgt_all, g_send, t_recv, way).wait_send()
+    for way in (0, 1, 2):
+        first(spack, src_all, f_send, s_recv, way).wait_send()
+
+    def sent(pushes, bits, ways, lo, hi):
+        def go(step, _):
+            for way in ways:
+                pushes(slot_of(side(bits), mix(g, step, grp_n)), way).wait_send()
+            return 0
+        lax.fori_loop(lo, hi, go, 0)
+
+    sent(t_push, 0, (1, 2), 1, grp_n)
+    sent(s_push, 0, (1, 2, 0), 1, grp_n)
+    sent(t_push, 2, (2,), 0, half)
+    sent(t_push, 4, (1,), half, grp_n)
+    sent(s_push, 2, (2, 0), 0, half)
+    sent(s_push, 4, (0,), 0, half)
+    sent(s_push, 4, (1, 0), half, grp_n)
+    sent(s_push, 2, (0,), half, grp_n)
+    sent(s_push, 6, (0,), 0, grp_n)
+    copy_s.wait()
+    copy_t.wait()
+
+
+def safe_kernel(grp_n, count, src_ref, tgt_ref, fast_ref, src_hbm, tgt_hbm, s_out, t_out,
+                raw_s, raw_t, src_all, tgt_all, cost, tcat, logb, u, v, loga, sems):
+    n_dev = src_all.shape[0]
+    points = n_dev * count
+    rep = LANES // count
+    chunks = points // LANES
+    wide = count + 1
+    s_out[...] = fast_ref[0:1, 0:count]
+    t_out[...] = fast_ref[1:2, 0:count]
+
+    @pl.when(jnp.logical_not(jnp.min(fast_ref[2:3, :]) >= FLOOR))
+    def _():
+        b, g = lax.axis_index("blk"), lax.axis_index("grp")
+        me = b * grp_n + g
+        copies = [pltpu.make_async_copy(x, y, sems.at[i]) for i, (x, y) in enumerate(
+            [(src_hbm, src_all), (tgt_hbm, tgt_all), (src_ref, raw_s), (tgt_ref, raw_t)])]
+        for c in copies:
+            c.start()
+        for c in copies:
+            c.wait()
+        eye = (lax.broadcasted_iota(jnp.int32, (count, LANES), 1) % count
+               == lax.broadcasted_iota(jnp.int32, (count, LANES), 0))
+        low = lax.broadcasted_iota(jnp.int32, (count, LANES), 1) < count
+
+        def target(r, _):
+            rows = pl.ds(pl.multiple_of(r * count, count), count)
+            block = tgt_all[r, 0:count, :]
+            tcat[rows, :] = block
+            mass = jnp.sum(jnp.where(eye & low, tgt_all[r, count:wide, :], 0.0), axis=1, keepdims=True)
+            square = jnp.sum(block * block, axis=1, keepdims=True)
+            mass = log2(jnp.broadcast_to(mass, (count, LANES)))
+            logb[rows, :] = mass
+            u[rows, :] = mass - ALPHA * square
+            return 0
+
+        lax.fori_loop(0, n_dev, target, 0)
+
+        def make_cost(k, _):
+            blocks = [src_all[k * rep + i, 0:count, :] for i in range(rep)]
+            loga[pl.ds(k, 1), :] = log2(sum(src_all[k * rep + i, count:wide, :] for i in range(rep)))
+            s = jnp.concatenate(blocks, axis=0) * (2.0 * ALPHA)
+
+            def rows_of(i, _):
+                rows = pl.ds(pl.multiple_of(i * LANES, LANES), LANES)
+                cost[k, rows, :] = lax.dot_general(
+                    tcat[rows, :], s, (((1,), (1,)), ((), ())),
+                    precision=lax.Precision.HIGHEST, preferred_element_type=jnp.float32)
+                return 0
+
+            return lax.fori_loop(0, points // LANES, rows_of, 0)
+
+        lax.fori_loop(0, chunks, make_cost, 0)
+
+        def source_step(k, _):
+            def block(i, carry):
+                m0, s0 = carry
+                rows = pl.ds(pl.multiple_of(i * LANES, LANES), LANES)
+                x = (cost[k, rows, :] + u[rows, :]).reshape(LANES // SUB, SUB, LANES)
+                m = jnp.maximum(m0, jnp.max(x, axis=0))
+                return m, s0 * exp2(m0 - m) + jnp.sum(exp2(x - m[None]), axis=0)
+
+            m, s = lax.fori_loop(0, points // LANES, block, (
+                jnp.full((SUB, LANES), -1e30, jnp.float32), jnp.zeros((SUB, LANES), jnp.float32)))
+            top = jnp.max(m, axis=0, keepdims=True)
+            total = jnp.sum(s * exp2(m - top), axis=0, keepdims=True)
+            v[pl.ds(k, 1), :] = loga[pl.ds(k, 1), :] - (top + log2(total))
+            return 0
+
+        def target_step(r, _):
+            rows = pl.ds(pl.multiple_of(r * SUB, SUB), SUB)
+            x = [cost[k, rows, :] + v[k : k + 1, :] for k in range(chunks)]
+            m = functools.reduce(jnp.maximum, x)
+            s = sum(exp2(y - m) for y in x)
+            top = jnp.max(m, axis=1, keepdims=True)
+            total = jnp.sum(s * exp2(m - top), axis=1, keepdims=True)
+            u[rows, :] = logb[rows, :] - (top + log2(total))
+            return 0
+
+        def iteration(t, _):
+            lax.fori_loop(0, chunks, source_step, 0)
+            lax.fori_loop(0, points // SUB, target_step, 0)
+            return 0
+
+        lax.fori_loop(0, ITERS, iteration, 0)
+
+        def to_lanes(column):
+            return jnp.sum(jnp.where(eye, column, 0.0), axis=0, keepdims=True)
+
+        src = raw_s[...]
+        row = pl.ds(me // rep, 1)
+        full = to_lanes(jnp.sum(src * src, axis=1, keepdims=True)) - (1.0 / ALPHA) * (loga[row, :] - v[row, :])
+        tgt = raw_t[...]
+        mine = pl.ds(pl.multiple_of(me * count, count), count)
+        second = to_lanes(jnp.sum(tgt * tgt, axis=1, keepdims=True) - (1.0 / ALPHA) * (logb[mine, :] - u[mine, :]))
+        picked = full[:, 0:count]
+        for i in range(1, rep):
+            picked = jnp.where(me % rep == i, full[:, i * count : (i + 1) * count], picked)
+        s_out[...] = picked
+        t_out[...] = second[:, 0:count]
+
+
+def fits(blk_n, grp_n, shape):
+    count, width = shape
+    points = blk_n * grp_n * count
+    return (blk_n == OCT and width == LANES and LANES % count == 0 and count % SUB == 0
+            and grp_n & (grp_n - 1) == 0 and grp_n > 1 and (grp_n * count) % LANES == 0
+            and (points // 2) % (MROWS * GROUP // SUB) == 0 and points * points * 4 <= BUDGET)
+
+
+def chip_device(blk_n, grp_n, source, target, source_mass, target_mass):
+    count = source.shape[0]
+    n_dev = blk_n * grp_n
+    points = n_dev * count
+    nt = points // 2
+    chunks = points // LANES
+    halves = grp_n * count // LANES
+    wide = count + 1
+    f32 = jnp.float32
+    vmem = pl.BlockSpec(memory_space=pltpu.VMEM)
+    hbm = pl.BlockSpec(memory_space=pl.ANY)
+    dma = pltpu.SemaphoreType.DMA
+    everything = jax.ShapeDtypeStruct((n_dev, wide, LANES), f32)
+    fast, src_hbm, tgt_hbm = pl.pallas_call(
+        functools.partial(chip_kernel, grp_n, count),
+        out_shape=(jax.ShapeDtypeStruct((SUB, LANES), f32), everything, everything),
+        in_specs=[vmem] * 4,
+        out_specs=(vmem, hbm, hbm),
+        scratch_shapes=[
+            pltpu.VMEM((n_dev, wide, LANES), f32),
+            pltpu.VMEM((n_dev, wide, LANES), f32),
+            pltpu.VMEM((wide, LANES), f32),
+            pltpu.VMEM((wide, LANES), f32),
+            pltpu.VMEM((nt, 2 * LANES), jnp.bfloat16),
+            pltpu.VMEM((nt // SUB, chunks, SUB, LANES), f32),
+            pltpu.VMEM((nt, LANES), f32),
+            pltpu.VMEM((nt, LANES), f32),
+            pltpu.VMEM((chunks, LANES), f32),
+            pltpu.VMEM((blk_n, 2 * halves, LANES), f32),
+            pltpu.VMEM((blk_n, 2 * halves, LANES), f32),
+            pltpu.VMEM((2, chunks + SUB, LANES), f32),
+            pltpu.VMEM((2, chunks + SUB, LANES), f32),
+            pltpu.VMEM((chunks, LANES), f32),
+            pltpu.VMEM((chunks, LANES), f32),
+            pltpu.VMEM((chunks, LANES), f32),
+            pltpu.VMEM((chunks, LANES), f32),
+            dma((grp_n,)), dma((3, n_dev)), dma((n_dev,)),
+            dma((grp_n,)), dma((3, n_dev)), dma((n_dev,)),
+            dma((blk_n,)), dma((blk_n,)), dma((2,)), dma((2,)), dma((2,)),
+        ],
+        compiler_params=pltpu.CompilerParams(
+            collective_id=0, has_side_effects=True, vmem_limit_bytes=62 * 2**20),
+    )(source, target, source_mass.reshape(1, count), target_mass.reshape(1, count))
+    row = jax.ShapeDtypeStruct((1, count), f32)
+    first, second = pl.pallas_call(
+        functools.partial(safe_kernel, grp_n, count),
+        out_shape=(row, row),
+        in_specs=[hbm, hbm, vmem, hbm, hbm],
+        out_specs=(vmem, vmem),
+        scratch_shapes=[
+            pltpu.VMEM((count, LANES), f32),
+            pltpu.VMEM((count, LANES), f32),
+            pltpu.VMEM((n_dev, wide, LANES), f32),
+            pltpu.VMEM((n_dev, wide, LANES), f32),
+            pltpu.VMEM((chunks, points, LANES), f32),
+            pltpu.VMEM((points, LANES), f32),
+            pltpu.VMEM((points, LANES), f32),
+            pltpu.VMEM((points, LANES), f32),
+            pltpu.VMEM((chunks, LANES), f32),
+            pltpu.VMEM((chunks, LANES), f32),
+            dma((4,)),
+        ],
+        compiler_params=pltpu.CompilerParams(vmem_limit_bytes=62 * 2**20),
+    )(source, target, fast, src_hbm, tgt_hbm)
+    return first.reshape(count), second.reshape(count)
+
+
 def solution(mesh):
     blk_n, grp_n = mesh.shape["blk"], mesh.shape["grp"]
     n_dev = blk_n * grp_n
 
-    def per_device(source, target, source_mass, target_mass):
+    def wide_device(source, target, source_mass, target_mass):
         count, width = source.shape
         points = n_dev * count
         part = OCT
@@ -331,7 +869,7 @@
         vmem = pl.BlockSpec(memory_space=pltpu.VMEM)
         dma = pltpu.SemaphoreType.DMA
         out = pl.pallas_call(
-            functools.partial(kernel, blk_n, grp_n, part, count, pieces),
+            functools.partial(wide_kernel, blk_n, grp_n, part, count, pieces),
             out_shape=jax.ShapeDtypeStruct((2, count), f32),
             in_specs=[vmem] * 4,
             out_specs=vmem,
@@ -358,6 +896,11 @@
         )(source, target, source_mass.reshape(1, count), target_mass.reshape(1, count))
         return out[0], out[1]
 
+    def per_device(source, target, source_mass, target_mass):
+        if fits(blk_n, grp_n, source.shape):
+            return chip_device(blk_n, grp_n, source, target, source_mass, target_mass)
+        return wide_device(source, target, source_mass, target_mass)
+
     both = P(("blk", "grp"))
     return jax.shard_map(
         per_device,

time: 59.8 us -> 56.3 us (0.941)
  Pallas kernels: 57.3 us -> 55.1 us
  local copies, waits for them, and re-layouts: 1.25 us -> 0 us
    pallas_call x1 -> x2, Pallas kernels: 57.3 us -> 55.1 us  [the longest x1 53.8 us: chip_device(): pl.pallas_call(functools.partial(chip_kernel, grp_n, count), out_shape=(j...]
    squeeze x1 -> x0, local copies, waits for them, and re-layouts: 1.25 us -> none  [per_device(): return (out[0], out[1])]
where the time goes in v1:
time: 56.3 us; the launch traced here: 55.8 us
  Pallas kernels  55.1 us (98%)
  between operations  0.64 us (1%)
    pallas_call x1, Pallas kernels, chip_device(): pl.pallas_call(functools.partial(chip_kernel, grp_n, count), out_shape=(j...  53.8 us
    pallas_call x1, Pallas kernels, chip_device(): pl.pallas_call(functools.partial(safe_kernel, grp_n, count), out_shape=(r...  1.35 us

profile of v1, /device:TPU:1, one launch (start us, length us, event | category | flops | bytes accessed | tf_op | source)
XLA Modules:
  0.0 55.8 jit_solution(1149119478197065812)
XLA Ops:
  0.6 53.8 %shard_map.59 = (f32[8,128]{1,0:T(8,128)}, f32[32,65,128]{2,1,0:T(8,128)}, f32[32,65,128]{2,1,0:T(8,128)}) custom-call(f32[64,128]{1,0:T(8,128)} %src_ref.3, f32[64,128]{1,0:T(8,128)} %tgt_ref.3, f32[1,64]{1,0:T(1,128)} %bitcast.4, f32[1,64]{1,0:T(1,128)} %bitcast.5), custom_call_target="tpu_custom_call" | custom-call | tf_op jit(solution)/shard_map/pallas_call | solution.py:799
  54.4 1.4 %shard_map.60 = (f32[1,64]{1,0:T(1,128)}, f32[1,64]{1,0:T(1,128)}) custom-call(f32[64,128]{1,0:T(8,128)} %src_ref.3, f32[64,128]{1,0:T(8,128)} %tgt_ref.3, f32[8,128]{1,0:T(8,128)} %get-tuple-element.7.fast_ref, f32[32,65,128]{2,1,0:T(8,128)} %get-tuple-element.8.src_hbm, f32[32,65,128]{2,1,0:T(8,128)} %get-tuple-element.9.tgt_hbm), custom_call_target="tpu_custom_call" | custom-call | tf_op jit(solution)/shard_map/pallas_call | solution.py:830
